TPU v7x, 256 devices: a whole 4x4x8 slice. The times are simulated.
256 devices in a mesh: site: 2 (over z_hi), row: 4 (over z_lo), col: 32 (over y, x, core).
Axes of the slice: x: 4, y: 4, z: 8 (z_hi: 2, z_lo: 4; z = z_hi * 4 + z_lo), core: 2. Of those that a mesh axis runs over, the one named last changes fastest.
Arguments:
- pair_array: bfloat16 [1024, 512, 128], P(('site', 'row'), 'col'), parts along dimension 0, may hold values from -6 to 6
- in_gain: float32 [128], replicated, may hold values from 0.25 to 1.75
- left_weight: bfloat16 [256, 128], P('site'), parts along dimension 0, may hold values from -0.5 to 0.5
- right_weight: bfloat16 [256, 128], P('site'), parts along dimension 0, may hold values from -0.5 to 0.5
- mid_gain: float32 [128], replicated, may hold values from 0.25 to 1.75
- out_weight: bfloat16 [256, 128], P('site'), parts along dimension 0, may hold values from -0.5 to 0.5
- out_gate: bfloat16 [256, 128], P('site'), parts along dimension 0, may hold values from -0.5 to 0.5
Outputs:
- triangle_out: bfloat16 [1024, 512, 128], P(('site', 'row'), 'col'), parts along dimension 0
There are 2 independent parts, one for each index of `site`. A program takes and returns all parts, laid end to end along the dimension named above; an argument that names none is the same for every part. Nothing has to cross between parts.
All inputs are finite; a program needn't handle non-finite values.
Results may differ from a plain program's by a relative error of at most 0.012.
Values may be sent and summed in bfloat16 or wider, within the bound.
No kernel may reach another device: no remote copies, remote signals or barrier semaphores. Data moves between devices by JAX's collectives and lax.ppermute only.
A program may use at most 64 MiB of HBM per device.

v0:
```python
import jax
import jax.numpy as jnp
from jax import lax
from jax.sharding import PartitionSpec as P


def norm_channels(values, channel_gain):
    centred = values - jnp.mean(values, axis=-1, keepdims=True)
    return (
        centred
        * lax.rsqrt(jnp.mean(centred * centred, axis=-1, keepdims=True) + 1e-05)
        * channel_gain
    )


def both_factors(pair_in, in_gain, left_weight, right_weight):
    ready = norm_channels(pair_in.astype(jnp.float32), in_gain).astype(jnp.bfloat16)
    ready = lax.optimization_barrier(ready)
    left = jnp.einsum("ijc,cd->ijd", ready, left_weight, preferred_element_type=jnp.float32)
    right = jnp.einsum("ijc,cd->ijd", ready, right_weight, preferred_element_type=jnp.float32)
    return (ready, left.astype(jnp.bfloat16), right.astype(jnp.bfloat16))


def finish_pair(mixed, ready, mid_gain, out_weight, out_gate):
    scaled = norm_channels(mixed.astype(jnp.float32), mid_gain).astype(jnp.bfloat16)
    scaled = lax.optimization_barrier(scaled)
    gate = jax.nn.sigmoid(
        jnp.einsum("ijc,cd->ijd", ready, out_gate, preferred_element_type=jnp.float32)
    )
    return (
        jnp.einsum("ijd,dc->ijc", scaled, out_weight, preferred_element_type=jnp.float32) * gate
    ).astype(jnp.bfloat16)


def body(pair_array, in_gain, left_weight, right_weight, mid_gain, out_weight, out_gate):
    ready, left, right = both_factors(pair_array, in_gain, left_weight, right_weight)
    count = pair_array.shape[0] * lax.axis_size("row")
    left_lines, right_lines = (
        lax.all_to_all(left, "row", split_axis=2, concat_axis=0, tiled=True),
        lax.all_to_all(right, "row", split_axis=2, concat_axis=0, tiled=True),
    )
    strip = jnp.einsum(
        "kid,kjd->ijd",
        lax.all_gather(left_lines, "col", axis=1, tiled=True),
        right_lines,
        preferred_element_type=jnp.float32,
    )
    strip = (strip * count ** (-0.5)).astype(jnp.bfloat16)
    mixed = lax.all_to_all(strip, "row", split_axis=0, concat_axis=2, tiled=True)
    return finish_pair(mixed, ready, mid_gain, out_weight, out_gate)


def solution(mesh):
    return jax.shard_map(
        body,
        mesh=mesh,
        in_specs=(
            P(("site", "row"), "col", None),
            P(),
            P("site", None),
            P("site", None),
            P(),
            P("site", None),
            P("site", None),
        ),
        out_specs=P(("site", "row"), "col", None),
        check_vma=False,
    )
```

profile of v0, /device:TPU:1, one launch (start us, length us, event | category | flops | bytes accessed | tf_op | source)
XLA Modules:
  0.0 160.3 jit_solution(11770206688560710799)
XLA Ops:
  6.5 0.0 copy-start
  6.5 0.0 all-gather.2.cloned.1.call-start
  6.5 1.4 convert_reduce_fusion
  7.9 0.1 copy.81
  8.0 0.1 copy.82
  8.1 1.7 %fusion.9 = f32[128,16]{1,0:T(8,128)S(1)} fusion(bf16[128,16,128]{2,1,0:T(8,128)(2,1)} %param.7, f32[128,16]{1,0:T(8,128)S(1)} %copy.82), kind=kLoop, calls=%fused_computation.15 | loop fusion | flops 1046528 | bytes 540672 | tf_op jit(solution)/shard_map/reduce_sum | solution.py:11
  9.8 0.1 copy.83
  9.9 0.1 copy.84
  10.0 1.7 %fusion.11 = bf16[128,16,128]{2,1,0:T(8,128)(2,1)S(1)} fusion(bf16[128,16,128]{2,1,0:T(8,128)(2,1)} %param.7, f32[128]{0:T(128)} %param.8, f32[128,16]{1,0:T(8,128)S(1)} %copy.84, f32[128,16]{1,0:T(8,128)S(1)} %copy.82), kind=kLoop, calls=%fused_computation.17 | loop fusion | flops 1310720 | bytes 1065472 | tf_op jit(solution)/shard_map/convert_element_type | solution.py:17
  11.6 0.0 copy-done
  11.7 0.3 convolution_convert_fusion
  12.0 0.4 copy.90
  12.4 19.9 %all_to_all.45 = bf16[128,16,128]{0,1,2:T(8,128)(2,1)S(1)} all-to-all(bf16[128,16,128]{0,1,2:T(8,128)(2,1)S(1)} %copy.90), channel_id=1, replica_groups=mesh['site'=2,'row'=4,'col'=32] {'row'}, dimensions={2} | all-to-all | bytes 1048576 | tf_op jit(solution)/shard_map/all_to_all | solution.py:39
  32.3 0.9 copy.115
  33.3 0.0 all-gather.2.cloned.1.call-update
  33.3 1.1 convolution_convert_fusion.1
  34.3 0.4 copy.86
  34.8 16.5 %all_to_all.46 = bf16[128,16,128]{0,1,2:T(8,128)(2,1)S(1)} all-to-all(bf16[128,16,128]{0,1,2:T(8,128)(2,1)S(1)} %copy.86), channel_id=1, replica_groups=mesh['site'=2,'row'=4,'col'=32] {'row'}, dimensions={2} | all-to-all | bytes 1048576 | tf_op jit(solution)/shard_map/all_to_all | solution.py:40
  51.2 61.5 %all-gather.2.cloned.1.call-done = bf16[512,512,32]{0,1,2:T(8,128)(2,1)} async-done(((bf16[512,16,32]{0,1,2:T(8,128)(2,1)}), bf16[512,512,32]{0,1,2:T(8,128)(2,1)}) %all-gather.2.cloned.1.call-update) | async-done | bytes 16777232 | tf_op jit(solution)/shard_map/all_gather | solution.py:44
  112.7 0.0 copy-start.2
  112.7 0.0 copy-start.1
  112.8 0.0 copy-start.3
  112.8 10.3 %fusion.8 = bf16[512,16,32]{0,1,2:T(8,128)(2,1)S(1)} fusion(bf16[512,512,32]{0,1,2:T(8,128)(2,1)} %all-gather.2.cloned.1.call-done, bf16[4,32,2,8,128]{4,3,2,1,0:T(8,128)(2,1)S(1)} %bitcast.44), kind=kOutput, calls=%fused_computation.14 | convolution fusion | flops 268959744 | bytes 17825792 | tf_op jit(solution)/shard_map/kid,kjd->ijd/dot_general | solution.py:42
  123.0 2.2 %copy.93 = bf16[512,16,32]{2,1,0:T(8,128)(2,1)S(1)} copy(bf16[512,16,32]{0,1,2:T(8,128)(2,1)S(1)} %fusion.8) | data formatting | bytes 1048576 | tf_op jit(solution)/shard_map/convert_element_type | solution.py:48
  125.2 2.2 %reshape.39 = bf16[4,2,32768]{2,1,0:T(2,128)(2,1)S(1)} reshape(bf16[512,16,32]{2,1,0:T(8,128)(2,1)S(1)} %copy.93) | data formatting | bytes 1048576
  127.4 18.5 %all_to_all.47 = bf16[4,2,32768]{2,1,0:T(2,128)(2,1)} all-to-all(bf16[4,2,32768]{2,1,0:T(2,128)(2,1)S(1)} %reshape.39), channel_id=1, replica_groups=mesh['site'=2,'row'=4,'col'=32] {'row'}, dimensions={0} | all-to-all | bytes 1048576 | tf_op jit(solution)/shard_map/all_to_all | solution.py:49
  145.9 2.9 %reshape.40 = bf16[512,16,32]{2,1,0:T(8,128)(2,1)S(1)} reshape(bf16[4,2,32768]{2,1,0:T(2,128)(2,1)} %all_to_all.47) | data formatting | bytes 1048576
  148.7 1.6 %copy.94 = bf16[512,16,32]{0,2,1:T(8,128)(2,1)S(1)} copy(bf16[512,16,32]{2,1,0:T(8,128)(2,1)S(1)} %reshape.40) | data formatting | bytes 1048576 | tf_op jit(solution)/shard_map/all_to_all | solution.py:49
  150.4 0.3 reshape.34
  150.7 0.1 bitcast_reduce_fusion
  150.9 0.3 multiply_reduce_fusion
  151.2 0.1 copy.95
  151.3 0.0 copy-done.2
  151.3 0.2 fusion.14
  151.5 0.0 copy-done.1
  151.5 0.3 fusion.21
  151.9 0.0 copy-done.3
  151.9 0.4 fusion.4
  152.3 1.1 copy.98
  (4 shorter events, 0.0 us)
Async XLA Ops:
  6.5 5.1 %copy-start = (bf16[128,128]{1,0:T(8,128)(2,1)S(1)}, bf16[128,128]{1,0:T(8,128)(2,1)}, u32[]{:S(2)}) copy-start(bf16[128,128]{1,0:T(8,128)(2,1)} %param.9) | copy-start | bytes 98308
  6.5 106.2 %all-gather.2.cloned.1.call-start = ((), (), s32[]{:S(2)}) async-start(), calls=%async_computation.3 | async-start | bytes 17301504 | tf_op jit(solution)/shard_map/all_gather | solution.py:44
  112.7 38.5 %copy-start.2 = (f32[128]{0:T(128)S(1)}, f32[128]{0:T(128)}, u32[]{:S(2)}) copy-start(f32[128]{0:T(128)} %param.11) | copy-start | bytes 1540
  112.7 38.8 %copy-start.1 = (bf16[128,128]{1,0:T(8,128)(2,1)S(1)}, bf16[128,128]{1,0:T(8,128)(2,1)}, u32[]{:S(2)}) copy-start(bf16[128,128]{1,0:T(8,128)(2,1)} %param.12) | copy-start | bytes 98308
  112.8 39.1 %copy-start.3 = (bf16[128,128]{1,0:T(8,128)(2,1)S(1)}, bf16[128,128]{1,0:T(8,128)(2,1)}, u32[]{:S(2)}) copy-start(bf16[128,128]{1,0:T(8,128)(2,1)} %param.13) | copy-start | bytes 98308
Sparse Core Ops, SparseCore 0:
  33.4 79.3 all-gather.1
where the time goes:
time: 161 us; the launch traced here: 160 us
  waiting for transfers between devices  61.5 us (38%)
  blocking collectives  54.9 us (34%)
  between operations  13.6 us (8%)
  local copies, waits for them, and re-layouts  12.6 us (8%)
  matrix products  12.4 us (8%)
  other arithmetic  5.38 us (3%)
    all_gather x1, waiting for transfers between devices, body(): lax.all_gather(left_lines, 'col', axis=1, tiled=True)  61.5 us
    all_to_all x1, blocking collectives, body(): lax.all_to_all(left, 'row', split_axis=2, concat_axis=0, tiled=True)  19.9 us
    all_to_all x1, blocking collectives, body(): lax.all_to_all(strip, 'row', split_axis=0, concat_axis=2, tiled=True)  18.5 us
    all_to_all x1, blocking collectives, body(): lax.all_to_all(right, 'row', split_axis=2, concat_axis=0, tiled=True)  16.5 us
    dot_general x1, matrix products, body(): jnp.einsum('kid,kjd->ijd', lax.all_gather(left_lines, 'col', axis=1, tile...  10.3 us
    unnamed x10, local copies, waits for them, and re-layouts  5.04 us
  transfers between devices with their start and end apart: 1, of which 1 were waited for; matrix products, arithmetic and copies ran while one was open for 1% of the time, Pallas kernels for 0%

commit v1 on v0

v1 whole, which is shorter than its diff:
```python
import functools

import jax
import jax.numpy as jnp
from jax import lax
from jax.experimental import pallas as pl
from jax.experimental.pallas import tpu as pltpu
from jax.sharding import PartitionSpec as P

VMEM = pl.BlockSpec(memory_space=pltpu.VMEM)
F32 = jnp.float32
BF16 = jnp.bfloat16


def front_kernel(x_ref, gain_ref, wl_ref, wr_ref, ready_ref, out_ref, rows_ref, tiles_ref):
    k, n, c = x_ref.shape
    d = wl_ref.shape[1]
    step = 16
    gain = gain_ref[...]

    def norm(s, _):
        x = x_ref[pl.ds(s * step, step)].reshape(step * n, c).astype(F32)
        centred = x - jnp.mean(x, axis=-1, keepdims=True)
        power = jnp.mean(centred * centred, axis=-1, keepdims=True)
        ready = (centred * lax.rsqrt(power + 1e-05) * gain).astype(BF16)
        ready_ref[pl.ds(s * step * n, step * n), :] = ready
        rows_ref[pl.ds(s * step * n, step * n), :] = ready.astype(F32)
        return 0

    lax.fori_loop(0, k // step, norm, 0)
    wl = wl_ref[...].astype(F32).T.astype(BF16)
    wr = wr_ref[...].astype(F32).T.astype(BF16)
    for i in range(n):
        ready = rows_ref[pl.ds(i, k, stride=n), :].astype(BF16)
        for side, w in ((0, wl), (1, wr)):
            tiles_ref[pl.ds(side * n + i, d, stride=2 * n), :] = lax.dot_general(
                w, ready, (((1,), (1,)), ((), ())), preferred_element_type=F32
            )

    def store(s, _):
        t = tiles_ref[pl.ds(s * 256, 256), :].astype(BF16)
        out_ref[pl.ds(s * (256 // (2 * n)), 256 // (2 * n))] = t.reshape(256 // (2 * n), 2 * n, k)
        return 0

    lax.fori_loop(0, d * 2 * n // 256, store, 0)


def middle_kernel(rows, scale, in_ref, out_ref):
    parts, n2, k = in_ref.shape
    n = n2 // 2
    cols = parts // rows
    for to in range(rows):
        total = jnp.zeros((cols * n, k), F32)
        for r in range(rows):
            left = in_ref[pl.ds(r * cols + to * (cols // rows), cols // rows), :n, :].reshape(cols // rows * n, k)
            right = in_ref[pl.ds(r * cols, cols), n:, :].reshape(cols * n, k)
            total += lax.dot_general(right, left, (((1,), (1,)), ((), ())), preferred_element_type=F32)
        out_ref[pl.ds(to * cols, cols)] = (total * scale).astype(BF16).reshape(cols, n, k)


def back_kernel(m_ref, ready_ref, gain_ref, w_ref, gate_ref, out_ref, rows_ref, sums_ref):
    d, n, k = m_ref.shape
    c = w_ref.shape[1]
    step = 8

    def total(s, acc):
        return acc + jnp.sum(m_ref[pl.ds(s * step, step)].astype(F32), axis=0)

    mean = lax.fori_loop(0, d // step, total, jnp.zeros((n, k), F32)) * (1.0 / d)

    def squares(s, acc):
        centred = m_ref[pl.ds(s * step, step)].astype(F32) - mean
        return acc + jnp.sum(centred * centred, axis=0)

    power = lax.fori_loop(0, d // step, squares, jnp.zeros((n, k), F32)) * (1.0 / d)
    root = lax.rsqrt(power + 1e-05)

    def scaled(s, _):
        centred = m_ref[pl.ds(s * step, step)].astype(F32) - mean
        rows_ref[pl.ds(s * step, step)] = centred * root
        return 0

    lax.fori_loop(0, d // step, scaled, 0)
    gain = gain_ref[...]
    w = w_ref[...]
    flat = rows_ref.reshape(d * n, k)
    for j in range(n):
        t = (flat[pl.ds(j, d, stride=n), :].T * gain).astype(BF16)
        sums_ref[pl.ds(j, k, stride=n), :] = jnp.dot(t, w, preferred_element_type=F32)
    g = gate_ref[...]

    def finish(s, _):
        at = pl.ds(s * 16 * n, 16 * n)
        gate = jax.nn.sigmoid(jnp.dot(ready_ref[at, :], g, preferred_element_type=F32))
        out_ref[pl.ds(s * 16, 16)] = (sums_ref[at, :] * gate).astype(BF16).reshape(16, n, c)
        return 0

    lax.fori_loop(0, k // 16, finish, 0)


def body(pair_array, in_gain, left_weight, right_weight, mid_gain, out_weight, out_gate):
    k, n, c = pair_array.shape
    d = left_weight.shape[1]
    rows, cols = lax.axis_size("row"), lax.axis_size("col")
    params = pltpu.CompilerParams(vmem_limit_bytes=32 << 20)
    ready, factors = pl.pallas_call(
        front_kernel,
        out_shape=(
            jax.ShapeDtypeStruct((k * n, c), BF16),
            jax.ShapeDtypeStruct((d, 2 * n, k), BF16),
        ),
        in_specs=[VMEM] * 4,
        out_specs=(VMEM, VMEM),
        scratch_shapes=[pltpu.VMEM((k * n, c), F32), pltpu.VMEM((d * 2 * n, k), F32)],
        compiler_params=params,
        name="front",
    )(pair_array, in_gain.reshape(1, c), left_weight, right_weight)
    factors = lax.all_to_all(factors, ("row", "col"), split_axis=0, concat_axis=0, tiled=True)
    mixed = pl.pallas_call(
        functools.partial(middle_kernel, rows, (k * rows) ** -0.5),
        out_shape=jax.ShapeDtypeStruct((rows * cols, n, k), BF16),
        in_specs=[VMEM],
        out_specs=VMEM,
        compiler_params=params,
        name="middle",
    )(factors)
    mixed = lax.all_to_all(mixed, ("row", "col"), split_axis=0, concat_axis=0, tiled=True)
    return pl.pallas_call(
        back_kernel,
        out_shape=jax.ShapeDtypeStruct((k, n, c), BF16),
        in_specs=[VMEM] * 5,
        out_specs=VMEM,
        scratch_shapes=[pltpu.VMEM((d, n, k), F32), pltpu.VMEM((k * n, c), F32)],
        compiler_params=params,
        name="back",
    )(mixed, ready, mid_gain.reshape(1, d), out_weight, out_gate)


def solution(mesh):
    return jax.shard_map(
        body,
        mesh=mesh,
        in_specs=(
            P(("site", "row"), "col", None),
            P(),
            P("site", None),
            P("site", None),
            P(),
            P("site", None),
            P("site", None),
        ),
        out_specs=P(("site", "row"), "col", None),
        check_vma=False,
    )
```

time: 161 us -> 79.1 us (0.49)
  waiting for transfers between devices: 61.5 us -> 0 us
  between operations: 13.6 us -> 0.04 us
  matrix products: 12.4 us -> 0 us
  blocking collectives: 54.9 us -> 67.1 us
  local copies, waits for them, and re-layouts: 12.6 us -> 3.87 us
  Pallas kernels: 0 us -> 7.7 us
  other arithmetic: 5.38 us -> 0 us
    all_gather x1 -> x0, waiting for transfers between devices: 61.5 us -> none  [body(): lax.all_gather(left_lines, 'col', axis=1, tiled=True)]
    dot_general x5 -> x0, matrix products: 12.4 us -> none  [the longest x1 10.3 us: body(): jnp.einsum('kid,kjd->ijd', lax.all_gather(left_lines, 'col', axis=1, tile...]
    all_to_all x3 -> x2, blocking collectives: 54.9 us -> 67.1 us  [the longest x1 43.1 us: body(): lax.all_to_all(factors, ('row', 'col'), split_axis=0, concat_axis=0, tile...]
    pallas_call x0 -> x3, Pallas kernels: none -> 7.7 us  [the longest x1 3.72 us: body(): pl.pallas_call(front_kernel, out_shape=(jax.ShapeDtypeStruct((k * n, c),...]
    convert_element_type x6 -> x0, local copies, waits for them, and re-layouts: 4.65 us -> none  [the longest x1 2.2 us: body(): strip = (strip * count ** (-0.5)).astype(jnp.bfloat16)]
    reduce_sum x4 -> x0, other arithmetic: 3.47 us -> none  [the longest x2 1.97 us: norm_channels(): jnp.mean(centred * centred, axis=-1, keepdims=True) + 1e-05]
    all_to_all x2 -> x0, local copies, waits for them, and re-layouts: 2.58 us -> none  [the longest x1 1.64 us: body(): lax.all_to_all(strip, 'row', split_axis=0, concat_axis=2, tiled=True)]
    convert_element_type x2 -> x0, other arithmetic: 1.88 us -> none  [the longest x1 1.65 us: both_factors(): norm_channels(pair_in.astype(jnp.float32), in_gain).astype(jnp.bfloat16)]
  transfers between devices with their start and end apart: 1 -> 0, of which waited for: 1 -> 0; matrix products, arithmetic and copies ran while one was open for 1% -> 0% of each run, Pallas kernels for 0% -> 0%
where the time goes in v1:
time: 79.1 us; the launch traced here: 78.7 us
  blocking collectives  67.1 us (85%)
  Pallas kernels  7.7 us (10%)
  local copies, waits for them, and re-layouts  3.87 us (5%)
    all_to_all x1, blocking collectives, body(): lax.all_to_all(factors, ('row', 'col'), split_axis=0, concat_axis=0, tile...  43.1 us
    all_to_all x1, blocking collectives, body(): lax.all_to_all(mixed, ('row', 'col'), split_axis=0, concat_axis=0, tiled=...  24 us
    unnamed x14, local copies, waits for them, and re-layouts  3.87 us
    pallas_call x1, Pallas kernels, body(): pl.pallas_call(front_kernel, out_shape=(jax.ShapeDtypeStruct((k * n, c),...  3.72 us
    pallas_call x1, Pallas kernels, body(): pl.pallas_call(back_kernel, out_shape=jax.ShapeDtypeStruct((k, n, c), BF1...  3.28 us

profile of v1, /device:TPU:1, one launch (start us, length us, event | category | flops | bytes accessed | tf_op | source)
XLA Modules:
  0.0 78.7 jit_solution(10822554458742904754)
XLA Ops:
  0.0 0.0 copy-start.6
  0.0 0.7 copy-done.6
  0.7 0.0 copy-start
  0.7 1.0 %copy-done = bf16[128,16,128]{2,1,0:T(8,128)(2,1)S(1)} copy-done((bf16[128,16,128]{2,1,0:T(8,128)(2,1)S(1)}, bf16[128,16,128]{2,1,0:T(8,128)(2,1)}, u32[]{:S(2)}) %copy-start) | copy-done | bytes 524312
  1.7 0.0 copy-start.3
  1.7 0.8 copy-done.3
  2.5 0.0 copy-start.4
  2.5 0.8 copy-done.4
  3.2 3.7 %front.1 = (bf16[2048,128]{1,0:T(8,128)(2,1)S(1)}, bf16[128,32,128]{2,1,0:T(8,128)(2,1)S(1)}) custom-call(bf16[128,16,128]{2,1,0:T(8,128)(2,1)S(1)} %copy-done, f32[1,128]{1,0:T(1,128)S(1)} %bitcast.3, bf16[128,128]{1,0:T(8,128)(2,1)S(1)} %copy-done.3, bf16[128,128]{1,0:T(8,128)(2,1)S(1)} %copy-done.4), custom_call_target="tpu_custom_call" | custom-call | tf_op jit(solution)/shard_map/front/pallas_call | solution.py:106
  6.9 43.1 %all_to_all.10.in_ref = bf16[128,32,128]{2,1,0:T(8,128)(2,1)S(1)} all-to-all(bf16[128,32,128]{2,1,0:T(8,128)(2,1)S(1)} %get-tuple-element.7), channel_id=1, replica_groups=mesh['site'=2,'row'=4,'col'=32] {'row','col'}, dimensions={0} | all-to-all | bytes 2097152 | tf_op jit(solution)/shard_map/all_to_all | solution.py:118
  50.1 0.7 middle.1
  50.8 0.0 copy-start.1
  50.8 0.0 copy-start.2
  50.8 24.0 %all_to_all.11.m_ref = bf16[128,16,128]{2,1,0:T(8,128)(2,1)S(1)} all-to-all(bf16[128,16,128]{2,1,0:T(8,128)(2,1)S(1)} %middle.1), channel_id=1, replica_groups=mesh['site'=2,'row'=4,'col'=32] {'row','col'}, dimensions={0} | all-to-all | bytes 1048576 | tf_op jit(solution)/shard_map/all_to_all | solution.py:127
  74.8 0.0 copy-start.5
  74.8 0.0 copy-done.1
  74.8 0.0 copy-done.2
  74.8 0.6 copy-done.5
  75.5 3.3 %back.1 = bf16[128,16,128]{2,1,0:T(8,128)(2,1)} custom-call(bf16[128,16,128]{2,1,0:T(8,128)(2,1)S(1)} %all_to_all.11.m_ref, bf16[2048,128]{1,0:T(8,128)(2,1)S(1)} %get-tuple-element.8.ready_ref, f32[1,128]{1,0:T(1,128)S(1)} %bitcast.2, bf16[128,128]{1,0:T(8,128)(2,1)S(1)} %copy-done.1, bf16[128,128]{1,0:T(8,128)(2,1)S(1)} %copy-done.2), custom_call_target="tpu_custom_call" | custom-call | tf_op jit(solution)/shard_map/back/pallas_call | solution.py:128
Async XLA Ops:
  0.0 0.7 copy-start.6
  0.7 1.0 %copy-start = (bf16[128,16,128]{2,1,0:T(8,128)(2,1)S(1)}, bf16[128,16,128]{2,1,0:T(8,128)(2,1)}, u32[]{:S(2)}) copy-start(bf16[128,16,128]{2,1,0:T(8,128)(2,1)} %x_ref.1) | copy-start | bytes 1572868
  1.7 0.8 copy-start.3
  2.5 0.8 copy-start.4
  50.8 24.0 %copy-start.1 = (bf16[128,128]{1,0:T(8,128)(2,1)S(1)}, bf16[128,128]{1,0:T(8,128)(2,1)}, u32[]{:S(2)}) copy-start(bf16[128,128]{1,0:T(8,128)(2,1)} %w_ref.1) | copy-start | bytes 98308
  50.8 24.0 %copy-start.2 = (bf16[128,128]{1,0:T(8,128)(2,1)S(1)}, bf16[128,128]{1,0:T(8,128)(2,1)}, u32[]{:S(2)}) copy-start(bf16[128,128]{1,0:T(8,128)(2,1)} %gate_ref.1) | copy-start | bytes 98308
  74.8 0.7 copy-start.5

commit v2 on v1

v2 whole, which is shorter than its diff:
```python
import functools

import jax
import jax.numpy as jnp
from jax import lax
from jax.experimental import pallas as pl
from jax.experimental.pallas import tpu as pltpu
from jax.sharding import PartitionSpec as P

VMEM = pl.BlockSpec(memory_space=pltpu.VMEM)
HBM = pl.BlockSpec(memory_space=pltpu.HBM)
F32 = jnp.float32
BF16 = jnp.bfloat16
PIECES = 2


def nt(a, b):
    return lax.dot_general(a, b, (((1,), (1,)), ((), ())), preferred_element_type=F32)


def in_hbm(x):
    return pltpu.with_memory_space_constraint(x, pltpu.HBM)


def front_kernel(x_hbm, gain_hbm, wl_hbm, wr_hbm, ready_ref, out_ref,
                 x_ref, gain_ref, wl_ref, wr_ref, rows_ref, tiles_ref, sems):
    k, n, c = x_ref.shape
    d = wl_ref.shape[1]
    pitch, wide = n + 1, 2 * n + 1
    part = k // PIECES
    pieces = [
        pltpu.make_async_copy(x_hbm.at[pl.ds(p * part, part)], x_ref.at[pl.ds(p * part, part)], sems.at[p])
        for p in range(PIECES)
    ]
    weights = [
        pltpu.make_async_copy(gain_hbm, gain_ref, sems.at[PIECES]),
        pltpu.make_async_copy(wl_hbm, wl_ref, sems.at[PIECES + 1]),
        pltpu.make_async_copy(wr_hbm, wr_ref, sems.at[PIECES + 2]),
    ]
    for copy in weights[:1] + pieces + weights[1:]:
        copy.start()
    weights[0].wait()
    gain = gain_ref[...]
    for p in range(PIECES):
        pieces[p].wait()
        x = x_ref[pl.ds(p * part, part)].reshape(part * n, c).astype(F32)
        centred = x - jnp.mean(x, axis=-1, keepdims=True)
        power = jnp.mean(centred * centred, axis=-1, keepdims=True)
        ready = (centred * lax.rsqrt(power + 1e-05) * gain).astype(BF16)
        ready_ref[pl.ds(p * part * n, part * n), :] = ready
        rows = ready.astype(F32)
        for q in range(part):
            rows_ref[pl.ds((p * part + q) * pitch, n), :] = rows[q * n : (q + 1) * n]
    weights[1].wait()
    weights[2].wait()
    w = jnp.concatenate([wl_ref[...].astype(F32).T, wr_ref[...].astype(F32).T], axis=0).astype(BF16)
    for i in range(n):
        both = nt(w, rows_ref[pl.ds(i, k, stride=pitch), :].astype(BF16))
        tiles_ref[pl.ds(i, d, stride=wide), :] = both[:d]
        tiles_ref[pl.ds(n + i, d, stride=wide), :] = both[d:]
    step = 32

    def store(s, _):
        for q in range(step):
            out_ref[s * step + q] = tiles_ref[pl.ds((s * step + q) * wide, 2 * n), :].astype(BF16)
        return 0

    lax.fori_loop(0, d // step, store, 0)


def gate_kernel(ready_ref, gate_hbm, gain_hbm, w_hbm, out_ref, gain_out_ref, w_out_ref, gate_ref, gain_ref, sems):
    copies = [
        pltpu.make_async_copy(gate_hbm, gate_ref, sems.at[0]),
        pltpu.make_async_copy(gain_hbm, gain_ref, sems.at[1]),
        pltpu.make_async_copy(w_hbm, w_out_ref, sems.at[2]),
    ]
    for copy in copies:
        copy.start()
    for copy in copies:
        copy.wait()
    g = gate_ref[...]
    step = 256

    def one(s, _):
        at = pl.ds(s * step, step)
        out_ref[at, :] = jax.nn.sigmoid(jnp.dot(ready_ref[at, :], g, preferred_element_type=F32))
        return 0

    lax.fori_loop(0, ready_ref.shape[0] // step, one, 0)
    gain_out_ref[...] = gain_ref[...]


def middle_kernel(rows, scale, in_ref, out_ref):
    parts, n2, k = in_ref.shape
    n = n2 // 2
    cols = parts // rows
    few = cols // rows
    right = jnp.concatenate([in_ref[pl.ds(r * cols, cols), n:, :].reshape(cols * n, k) for r in range(rows)], axis=1)
    for to in range(rows):
        left = jnp.concatenate(
            [
                in_ref[pl.ds(r * cols + to * few, few), :n, :].reshape(few * n, k).astype(F32).T.astype(BF16)
                for r in range(rows)
            ],
            axis=0,
        )
        total = jnp.dot(right, left, preferred_element_type=F32) * scale
        out_ref[pl.ds(to * cols, cols)] = total.astype(BF16).reshape(cols, n, k)


def back_kernel(m_ref, gate_ref, gain_ref, w_ref, out_hbm, rows_ref, sums_ref, out_ref, sems):
    d, n, k = m_ref.shape
    pitch = n + 1
    step = 32

    def total(s, acc):
        return acc + jnp.sum(m_ref[pl.ds(s * step, step)].astype(F32), axis=0)

    mean = lax.fori_loop(0, d // step, total, jnp.zeros((n, k), F32)) * (1.0 / d)

    def squares(s, acc):
        centred = m_ref[pl.ds(s * step, step)].astype(F32) - mean
        return acc + jnp.sum(centred * centred, axis=0)

    power = lax.fori_loop(0, d // step, squares, jnp.zeros((n, k), F32)) * (1.0 / d)
    root = lax.rsqrt(power + 1e-05)

    def scaled(s, _):
        for q in range(step):
            centred = m_ref[s * step + q].astype(F32) - mean
            rows_ref[pl.ds((s * step + q) * pitch, n), :] = centred * root
        return 0

    lax.fori_loop(0, d // step, scaled, 0)
    w = w_ref[...]
    gain = gain_ref[...]
    for j in range(n):
        t = (rows_ref[pl.ds(j, d, stride=pitch), :].T * gain).astype(BF16)
        sums_ref[pl.ds(j, k, stride=pitch), :] = jnp.dot(t, w, preferred_element_type=F32)
    part = k // PIECES
    copies = []
    for p in range(PIECES):

        def finish(s, _):
            for q in range(step):
                at = p * part + s * step + q
                out_ref[at] = (sums_ref[pl.ds(at * pitch, n), :] * gate_ref[pl.ds(at * n, n), :]).astype(BF16)
            return 0

        lax.fori_loop(0, part // step, finish, 0)
        copy = pltpu.make_async_copy(
            out_ref.at[pl.ds(p * part, part)], out_hbm.at[pl.ds(p * part, part)], sems.at[p]
        )
        copy.start()
        copies.append(copy)
    for copy in copies:
        copy.wait()


def body(pair_array, in_gain, left_weight, right_weight, mid_gain, out_weight, out_gate):
    k, n, c = pair_array.shape
    d = left_weight.shape[1]
    rows, cols = lax.axis_size("row"), lax.axis_size("col")
    params = pltpu.CompilerParams(vmem_limit_bytes=32 << 20)
    ready, factors = pl.pallas_call(
        front_kernel,
        out_shape=(
            jax.ShapeDtypeStruct((k * n, c), BF16),
            jax.ShapeDtypeStruct((d, 2 * n, k), BF16),
        ),
        in_specs=[HBM] * 4,
        out_specs=(VMEM, VMEM),
        scratch_shapes=[
            pltpu.VMEM((k, n, c), BF16),
            pltpu.VMEM((1, c), F32),
            pltpu.VMEM((c, d), BF16),
            pltpu.VMEM((c, d), BF16),
            pltpu.VMEM((k * (n + 1), c), F32),
            pltpu.VMEM((d * (2 * n + 1), k), F32),
            pltpu.SemaphoreType.DMA((PIECES + 3,)),
        ],
        compiler_params=params,
        name="front",
    )(in_hbm(pair_array), in_hbm(in_gain.reshape(1, c)), in_hbm(left_weight), in_hbm(right_weight))
    factors = lax.all_to_all(factors, ("row", "col"), split_axis=0, concat_axis=0, tiled=True)
    gate, gain, weight = pl.pallas_call(
        gate_kernel,
        out_shape=(
            jax.ShapeDtypeStruct((k * n, c), F32),
            jax.ShapeDtypeStruct((1, d), F32),
            jax.ShapeDtypeStruct((d, c), BF16),
        ),
        in_specs=[VMEM, HBM, HBM, HBM],
        out_specs=(VMEM, VMEM, VMEM),
        scratch_shapes=[
            pltpu.VMEM((c, c), BF16),
            pltpu.VMEM((1, d), F32),
            pltpu.SemaphoreType.DMA((3,)),
        ],
        compiler_params=params,
        cost_estimate=pl.CostEstimate(flops=4_000_000_000, bytes_accessed=2 << 20, transcendentals=k * n * c),
        name="gate",
    )(ready, in_hbm(out_gate), in_hbm(mid_gain.reshape(1, d)), in_hbm(out_weight))
    mixed = pl.pallas_call(
        functools.partial(middle_kernel, rows, (k * rows) ** -0.5),
        out_shape=pltpu.VMEM((rows * cols, n, k), BF16),
        in_specs=[VMEM],
        out_specs=VMEM,
        compiler_params=params,
        name="middle",
    )(factors)
    mixed = lax.all_to_all(mixed, ("row", "col"), split_axis=0, concat_axis=0, tiled=True)
    return pl.pallas_call(
        back_kernel,
        out_shape=jax.ShapeDtypeStruct((k, n, c), BF16),
        in_specs=[VMEM] * 4,
        out_specs=HBM,
        scratch_shapes=[
            pltpu.VMEM((d * (n + 1), k), F32),
            pltpu.VMEM((k * (n + 1), c), F32),
            pltpu.VMEM((k, n, c), BF16),
            pltpu.SemaphoreType.DMA((PIECES,)),
        ],
        compiler_params=params,
        name="back",
    )(mixed, gate, gain, weight)


def solution(mesh):
    return jax.shard_map(
        body,
        mesh=mesh,
        in_specs=(
            P(("site", "row"), "col", None),
            P(),
            P("site", None),
            P("site", None),
            P(),
            P("site", None),
            P("site", None),
        ),
        out_specs=P(("site", "row"), "col", None),
        check_vma=False,
    )
```

time: 79.1 us -> 73.8 us (0.933)
  blocking collectives: 67.1 us -> 43.1 us
  waiting for transfers between devices: 0 us -> 16.2 us
  starting transfers between devices: 0 us -> 6.37 us
  local copies, waits for them, and re-layouts: 3.87 us -> 0 us
    all_to_all x1 -> x0, blocking collectives: 24 us -> none  [body(): lax.all_to_all(mixed, ('row', 'col'), split_axis=0, concat_axis=0, tiled=...]
    all_to_all x0 -> x1, waiting for transfers between devices: none -> 16.2 us  [body(): lax.all_to_all(mixed, ('row', 'col'), split_axis=0, concat_axis=0, tiled=...]
    all_to_all x0 -> x1, starting transfers between devices: none -> 6.37 us  [body(): lax.all_to_all(mixed, ('row', 'col'), split_axis=0, concat_axis=0, tiled=...]
    unnamed x14 -> x0, local copies, waits for them, and re-layouts: 3.87 us -> none
    pallas_call x0 -> x1, Pallas kernels: none -> 2.1 us  [body(): pl.pallas_call(gate_kernel, out_shape=(jax.ShapeDtypeStruct((k * n, c), F...]
    pallas_call x1, Pallas kernels: 3.28 us -> 1.75 us  [body(): pl.pallas_call(back_kernel, out_shape=jax.ShapeDtypeStruct((k, n, c), BF1...]
    pallas_call x1, Pallas kernels: 3.72 us -> 2.32 us  [body(): pl.pallas_call(front_kernel, out_shape=(jax.ShapeDtypeStruct((k * n, c),...]
    pallas_call x1, Pallas kernels: 0.7 us -> 1.61 us  [body(): pl.pallas_call(functools.partial(middle_kernel, rows, (k * rows) ** (-0.5...]
  transfers between devices with their start and end apart: 0 -> 1, of which waited for: 0 -> 1; matrix products, arithmetic and copies ran while one was open for 0% -> 0% of each run, Pallas kernels for 0% -> 3%
where the time goes in v2:
time: 73.8 us; the launch traced here: 73.5 us
  blocking collectives  43.1 us (58%)
  waiting for transfers between devices  16.2 us (22%)
  Pallas kernels  7.78 us (11%)
  starting transfers between devices  6.37 us (9%)
    all_to_all x1, blocking collectives, body(): lax.all_to_all(factors, ('row', 'col'), split_axis=0, concat_axis=0, tile...  43.1 us
    all_to_all x1, waiting for transfers between devices, body(): lax.all_to_all(mixed, ('row', 'col'), split_axis=0, concat_axis=0, tiled=...  16.2 us
    all_to_all x1, starting transfers between devices, body(): lax.all_to_all(mixed, ('row', 'col'), split_axis=0, concat_axis=0, tiled=...  6.37 us
    pallas_call x1, Pallas kernels, body(): pl.pallas_call(front_kernel, out_shape=(jax.ShapeDtypeStruct((k * n, c),...  2.32 us
    pallas_call x1, Pallas kernels, body(): pl.pallas_call(gate_kernel, out_shape=(jax.ShapeDtypeStruct((k * n, c), F...  2.1 us
    pallas_call x1, Pallas kernels, body(): pl.pallas_call(back_kernel, out_shape=jax.ShapeDtypeStruct((k, n, c), BF1...  1.75 us
    pallas_call x1, Pallas kernels, body(): pl.pallas_call(functools.partial(middle_kernel, rows, (k * rows) ** (-0.5...  1.61 us
  transfers between devices with their start and end apart: 1, of which 1 were waited for; matrix products, arithmetic and copies ran while one was open for 0% of the time, Pallas kernels for 3%

profile of v2, /device:TPU:1, one launch (start us, length us, event | category | flops | bytes accessed | tf_op | source)
XLA Modules:
  0.0 73.5 jit_solution(3782204771354704972)
XLA Ops:
  0.0 2.3 %front.1 = (bf16[2048,128]{1,0:T(8,128)(2,1)S(1)}, bf16[128,32,128]{2,1,0:T(8,128)(2,1)S(1)}) custom-call(bf16[128,16,128]{2,1,0:T(8,128)(2,1)} %x_hbm.1, f32[1,128]{1,0:T(1,128)} %bitcast.2, bf16[128,128]{1,0:T(8,128)(2,1)} %wl_hbm.1, bf16[128,128]{1,0:T(8,128)(2,1)} %wr_hbm.1), custom_call_target="tpu_custom_call" | custom-call | tf_op jit(solution)/shard_map/front/pallas_call | solution.py:165
  2.3 43.1 %all_to_all.10.in_ref = bf16[128,32,128]{2,1,0:T(8,128)(2,1)S(1)} all-to-all(bf16[128,32,128]{2,1,0:T(8,128)(2,1)S(1)} %get-tuple-element.10), channel_id=1, replica_groups=mesh['site'=2,'row'=4,'col'=32] {'row','col'}, dimensions={0} | all-to-all | bytes 2097152 | tf_op jit(solution)/shard_map/all_to_all | solution.py:185
  45.4 1.6 %middle.1 = bf16[128,16,128]{2,1,0:T(8,128)(2,1)} custom-call(bf16[128,32,128]{2,1,0:T(8,128)(2,1)S(1)} %all_to_all.10.in_ref), custom_call_target="tpu_custom_call" | custom-call | tf_op jit(solution)/shard_map/middle/pallas_call | solution.py:204
  47.1 6.4 %all-to-all-start.1 = ((bf16[128,16,128]{2,1,0:T(8,128)(2,1)}), bf16[128,16,128]{2,1,0:T(8,128)(2,1)S(1)}, u32[]{:S(2)}, u32[]{:S(2)}) async-start(bf16[128,16,128]{2,1,0:T(8,128)(2,1)} %middle.1), calls=%async_computation.1 | async-start | bytes 1048576 | tf_op jit(solution)/shard_map/all_to_all | solution.py:212
  53.4 2.1 %gate.1 = (f32[2048,128]{1,0:T(8,128)S(1)}, f32[1,128]{1,0:T(1,128)S(1)}, bf16[128,128]{1,0:T(8,128)(2,1)S(1)}) custom-call(bf16[2048,128]{1,0:T(8,128)(2,1)S(1)} %get-tuple-element.11.ready_ref, bf16[128,128]{1,0:T(8,128)(2,1)} %gate_hbm.1, f32[1,128]{1,0:T(1,128)} %bitcast.3, bf16[128,128]{1,0:T(8,128)(2,1)} %w_hbm.1), custom_call_target="tpu_custom_call" | custom-call | flops 4000000000 | bytes 2097152 | tf_op jit(solution)/shard_map/gate/pallas_call | solution.py:186
  55.5 16.2 %all-to-all-done.1.m_ref = bf16[128,16,128]{2,1,0:T(8,128)(2,1)S(1)} async-done(((bf16[128,16,128]{2,1,0:T(8,128)(2,1)}), bf16[128,16,128]{2,1,0:T(8,128)(2,1)S(1)}, u32[]{:S(2)}, u32[]{:S(2)}) %all-to-all-start.1) | async-done | bytes 524320 | tf_op jit(solution)/shard_map/all_to_all | solution.py:212
  71.7 1.7 %back.1 = bf16[128,16,128]{2,1,0:T(8,128)(2,1)} custom-call(bf16[128,16,128]{2,1,0:T(8,128)(2,1)S(1)} %all-to-all-done.1.m_ref, f32[2048,128]{1,0:T(8,128)S(1)} %get-tuple-element.12.gate_ref, f32[1,128]{1,0:T(1,128)S(1)} %get-tuple-element.13.gain_ref, bf16[128,128]{1,0:T(8,128)(2,1)S(1)} %get-tuple-element.14.w_ref), custom_call_target="tpu_custom_call" | custom-call | tf_op jit(solution)/shard_map/back/pallas_call | solution.py:213
Async XLA Ops:
  47.1 24.7 %all-to-all-start.1 = ((bf16[128,16,128]{2,1,0:T(8,128)(2,1)}), bf16[128,16,128]{2,1,0:T(8,128)(2,1)S(1)}, u32[]{:S(2)}, u32[]{:S(2)}) async-start(bf16[128,16,128]{2,1,0:T(8,128)(2,1)} %middle.1), calls=%async_computation.1 | async-start | bytes 1048576 | tf_op jit(solution)/shard_map/all_to_all | solution.py:212

commit v3 on v2

--- a/solution.py
+++ b/solution.py
@@ -90,22 +90,24 @@
     gain_out_ref[...] = gain_ref[...]
 
 
-def middle_kernel(rows, scale, in_ref, out_ref):
-    parts, n2, k = in_ref.shape
-    n = n2 // 2
-    cols = parts // rows
-    few = cols // rows
-    right = jnp.concatenate([in_ref[pl.ds(r * cols, cols), n:, :].reshape(cols * n, k) for r in range(rows)], axis=1)
-    for to in range(rows):
-        left = jnp.concatenate(
-            [
-                in_ref[pl.ds(r * cols + to * few, few), :n, :].reshape(few * n, k).astype(F32).T.astype(BF16)
-                for r in range(rows)
-            ],
-            axis=0,
+def middle_kernel(rows, scale, own_ref, other_ref, out_ref):
+    chips, two, n, k = other_ref.shape
+    per = chips // rows
+    few = per // rows
+    for dd in range(two):
+        right = jnp.concatenate(
+            [own_ref[pl.ds(r * per, per), dd, n:, :].reshape(per * n, k) for r in range(rows)], axis=1
         )
-        total = jnp.dot(right, left, preferred_element_type=F32) * scale
-        out_ref[pl.ds(to * cols, cols)] = total.astype(BF16).reshape(cols, n, k)
+        for to in range(rows):
+            left = []
+            for r in range(rows):
+                at = pl.ds(r * per + to * few, few)
+                both = jnp.concatenate(
+                    [own_ref[at, dd, :n, :].reshape(few * n, k), other_ref[at, dd].reshape(few * n, k)], axis=0
+                )
+                left.append(both.astype(F32).T.astype(BF16))
+            total = jnp.dot(right, jnp.concatenate(left, axis=0), preferred_element_type=F32) * scale
+            out_ref[pl.ds(to * per, per), dd] = total.astype(BF16).reshape(per, n, k)
 
 
 def back_kernel(m_ref, gate_ref, gain_ref, w_ref, out_hbm, rows_ref, sums_ref, out_ref, sems):
@@ -134,9 +136,15 @@
     lax.fori_loop(0, d // step, scaled, 0)
     w = w_ref[...]
     gain = gain_ref[...]
+    core = lax.rem(lax.axis_index("col"), 2)
     for j in range(n):
         t = (rows_ref[pl.ds(j, d, stride=pitch), :].T * gain).astype(BF16)
-        sums_ref[pl.ds(j, k, stride=pitch), :] = jnp.dot(t, w, preferred_element_type=F32)
+        sums = jnp.dot(t, w, preferred_element_type=F32)
+        for h in range(2):
+            for q in range(k // (2 * n)):
+                at = (2 * q + (1 - core if h else core)) * n * pitch + j
+                block = h * (k // 2) + q * n
+                sums_ref[pl.ds(at, n, stride=pitch), :] = sums[block : block + n]
     part = k // PIECES
     copies = []
     for p in range(PIECES):
@@ -182,7 +190,16 @@
         compiler_params=params,
         name="front",
     )(in_hbm(pair_array), in_hbm(in_gain.reshape(1, c)), in_hbm(left_weight), in_hbm(right_weight))
-    factors = lax.all_to_all(factors, ("row", "col"), split_axis=0, concat_axis=0, tiled=True)
+    same_core = [[r * cols + q * 2 + core for r in range(rows) for q in range(cols // 2)] for core in range(2)]
+    chips = rows * cols // 2
+
+    def exchange(x):
+        return lax.all_to_all(
+            x, ("row", "col"), split_axis=0, concat_axis=0, tiled=True, axis_index_groups=same_core
+        )
+
+    factors = exchange(factors).reshape(chips, 2, 2 * n, k)
+    other = lax.ppermute(factors[:, :, :n], "col", [(i, i ^ 1) for i in range(cols)])
     gate, gain, weight = pl.pallas_call(
         gate_kernel,
         out_shape=(
@@ -201,15 +218,16 @@
         cost_estimate=pl.CostEstimate(flops=4_000_000_000, bytes_accessed=2 << 20, transcendentals=k * n * c),
         name="gate",
     )(ready, in_hbm(out_gate), in_hbm(mid_gain.reshape(1, d)), in_hbm(out_weight))
+    factors, other, gate, gain, weight = lax.optimization_barrier((factors, other, gate, gain, weight))
     mixed = pl.pallas_call(
         functools.partial(middle_kernel, rows, (k * rows) ** -0.5),
-        out_shape=pltpu.VMEM((rows * cols, n, k), BF16),
-        in_specs=[VMEM],
+        out_shape=jax.ShapeDtypeStruct((chips, 2, n, k), BF16),
+        in_specs=[VMEM] * 2,
         out_specs=VMEM,
         compiler_params=params,
         name="middle",
-    )(factors)
-    mixed = lax.all_to_all(mixed, ("row", "col"), split_axis=0, concat_axis=0, tiled=True)
+    )(factors, other)
+    mixed = exchange(mixed.reshape(d, n, k))
     return pl.pallas_call(
         back_kernel,
         out_shape=jax.ShapeDtypeStruct((k, n, c), BF16),

time: 73.8 us -> 71.1 us (0.963)
  blocking collectives: 43.1 us -> 61.1 us
  waiting for transfers between devices: 16.2 us -> 0.01 us
  starting transfers between devices: 6.37 us -> 2.66 us
  Pallas kernels: 7.78 us -> 6.97 us
    all_to_all x1 -> x2, blocking collectives: 43.1 us -> 61.1 us  [exchange(): lax.all_to_all(x, ('row', 'col'), split_axis=0, concat_axis=0, tiled=True...]
    all_to_all x1 -> x0, waiting for transfers between devices: 16.2 us -> none  [body(): lax.all_to_all(mixed, ('row', 'col'), split_axis=0, concat_axis=0, tiled=...]
    all_to_all x1 -> x0, starting transfers between devices: 6.37 us -> none  [body(): lax.all_to_all(mixed, ('row', 'col'), split_axis=0, concat_axis=0, tiled=...]
    ppermute x0 -> x1, starting transfers between devices: none -> 2.66 us  [body(): lax.ppermute(factors[:, :, :n], 'col', [(i, i ^ 1) for i in range(cols)])]
    pallas_call x1, Pallas kernels: 1.61 us -> 0.8 us  [body(): pl.pallas_call(functools.partial(middle_kernel, rows, (k * rows) ** (-0.5...]
  transfers between devices with their start and end apart: 1 -> 1, of which waited for: 1 -> 0; matrix products, arithmetic and copies ran while one was open for 0% -> 0% of each run, Pallas kernels for 3% -> 3%
where the time goes in v3:
time: 71.1 us; the launch traced here: 70.8 us
  blocking collectives  61.1 us (86%)
  Pallas kernels  6.97 us (10%)
  starting transfers between devices  2.66 us (4%)
    all_to_all x2, blocking collectives, exchange(): lax.all_to_all(x, ('row', 'col'), split_axis=0, concat_axis=0, tiled=True...  61.1 us
    ppermute x1, starting transfers between devices, body(): lax.ppermute(factors[:, :, :n], 'col', [(i, i ^ 1) for i in range(cols)])  2.66 us
    pallas_call x1, Pallas kernels, body(): pl.pallas_call(front_kernel, out_shape=(jax.ShapeDtypeStruct((k * n, c),...  2.32 us
    pallas_call x1, Pallas kernels, body(): pl.pallas_call(gate_kernel, out_shape=(jax.ShapeDtypeStruct((k * n, c), F...  2.1 us
    pallas_call x1, Pallas kernels, body(): pl.pallas_call(back_kernel, out_shape=jax.ShapeDtypeStruct((k, n, c), BF1...  1.75 us
  transfers between devices with their start and end apart: 1, of which 0 were waited for; matrix products, arithmetic and copies ran while one was open for 0% of the time, Pallas kernels for 3%

profile of v3, /device:TPU:1, one launch (start us, length us, event | category | flops | bytes accessed | tf_op | source)
XLA Modules:
  0.0 70.8 jit_solution(6982575326391673898)
XLA Ops:
  0.0 2.3 %front.1 = (bf16[2048,128]{1,0:T(8,128)(2,1)S(1)}, bf16[128,32,128]{2,1,0:T(8,128)(2,1)S(1)}) custom-call(bf16[128,16,128]{2,1,0:T(8,128)(2,1)} %x_hbm.1, f32[1,128]{1,0:T(1,128)} %bitcast.7, bf16[128,128]{1,0:T(8,128)(2,1)} %wl_hbm.1, bf16[128,128]{1,0:T(8,128)(2,1)} %wr_hbm.1), custom_call_target="tpu_custom_call" | custom-call | tf_op jit(solution)/shard_map/front/pallas_call | solution.py:173
  2.3 39.6 %all_to_all.10 = bf16[128,32,128]{2,1,0:T(8,128)(2,1)S(1)} all-to-all(bf16[128,32,128]{2,1,0:T(8,128)(2,1)S(1)} %get-tuple-element.15), channel_id=1, replica_groups={{0,2,4,6,8,10,12,14,16,18,20,22,24,26,28,30,32,34,36,38,40,42,44,46,48,..., dimensions={0} | all-to-all | bytes 2097152 | tf_op jit(solution)/shard_map/all_to_all | solution.py:197
  42.0 2.7 %collective-permute-start = (bf16[64,2,16,128]{3,2,1,0:T(8,128)(2,1)S(1)}, bf16[64,2,16,128]{3,2,1,0:T(8,128)(2,1)S(1)}, u32[]{:S(2)}, u32[]{:S(2)}) collective-permute-start(bf16[64,2,16,128]{3,2,1,0:T(8,128)(2,1)S(1)} %slice.4), channel_id=1, source_target_pairs={{0,1},{1,0},{2,3},{3,2},{4,5},{5,4},{6,7},{7,6},{8,9},{9,8},{10,11... | collective-permute-start | bytes 1572872 | tf_op jit(solution)/shard_map/ppermute | solution.py:202
  44.7 2.1 %gate.1 = (f32[2048,128]{1,0:T(8,128)S(1)}, f32[1,128]{1,0:T(1,128)S(1)}, bf16[128,128]{1,0:T(8,128)(2,1)S(1)}) custom-call(bf16[2048,128]{1,0:T(8,128)(2,1)S(1)} %get-tuple-element.16.ready_ref, bf16[128,128]{1,0:T(8,128)(2,1)} %gate_hbm.1, f32[1,128]{1,0:T(1,128)} %bitcast.8, bf16[128,128]{1,0:T(8,128)(2,1)} %w_hbm.1), custom_call_target="tpu_custom_call" | custom-call | flops 4000000000 | bytes 2097152 | tf_op jit(solution)/shard_map/gate/pallas_call | solution.py:203
  46.8 0.0 collective-permute-done.other_ref
  46.8 0.8 %middle.1 = bf16[64,2,16,128]{3,2,1,0:T(8,128)(2,1)S(1)} custom-call(bf16[64,2,32,128]{3,2,1,0:T(8,128)(2,1)S(1)} %bitcast.5, bf16[64,2,16,128]{3,2,1,0:T(8,128)(2,1)S(1)} %collective-permute-done.other_ref), custom_call_target="tpu_custom_call" | custom-call | tf_op jit(solution)/shard_map/middle/pallas_call | solution.py:222
  47.6 21.5 %all_to_all.11.m_ref = bf16[128,16,128]{2,1,0:T(8,128)(2,1)S(1)} all-to-all(bf16[128,16,128]{2,1,0:T(8,128)(2,1)S(1)} %bitcast.6), channel_id=1, replica_groups={{0,2,4,6,8,10,12,14,16,18,20,22,24,26,28,30,32,34,36,38,40,42,44,46,48,..., dimensions={0} | all-to-all | bytes 1048576 | tf_op jit(solution)/shard_map/all_to_all | solution.py:197
  69.1 1.7 %back.1 = bf16[128,16,128]{2,1,0:T(8,128)(2,1)} custom-call(bf16[128,16,128]{2,1,0:T(8,128)(2,1)S(1)} %all_to_all.11.m_ref, f32[2048,128]{1,0:T(8,128)S(1)} %get-tuple-element.22.gate_ref, f32[1,128]{1,0:T(1,128)S(1)} %get-tuple-element.23.gain_ref, bf16[128,128]{1,0:T(8,128)(2,1)S(1)} %get-tuple-element.24.w_ref), custom_call_target="tpu_custom_call" | custom-call | tf_op jit(solution)/shard_map/back/pallas_call | solution.py:231
  (1 shorter events, 0.0 us)
Async XLA Ops:
  42.0 4.8 %collective-permute-start = (bf16[64,2,16,128]{3,2,1,0:T(8,128)(2,1)S(1)}, bf16[64,2,16,128]{3,2,1,0:T(8,128)(2,1)S(1)}, u32[]{:S(2)}, u32[]{:S(2)}) collective-permute-start(bf16[64,2,16,128]{3,2,1,0:T(8,128)(2,1)S(1)} %slice.4), channel_id=1, source_target_pairs={{0,1},{1,0},{2,3},{3,2},{4,5},{5,4},{6,7},{7,6},{8,9},{9,8},{10,11... | collective-permute-start | bytes 1572872 | tf_op jit(solution)/shard_map/ppermute | solution.py:202

commit v4 on v3

--- a/solution.py
+++ b/solution.py
@@ -91,46 +91,55 @@
 
 
 def middle_kernel(rows, scale, own_ref, other_ref, out_ref):
-    chips, two, n, k = other_ref.shape
-    per = chips // rows
-    few = per // rows
-    for dd in range(two):
+    chips, per, n, k = other_ref.shape
+    halves = rows // 2
+    plane = chips // halves
+    few = plane // rows
+    for dd in range(per):
         right = jnp.concatenate(
-            [own_ref[pl.ds(r * per, per), dd, n:, :].reshape(per * n, k) for r in range(rows)], axis=1
+            [own_ref[pl.ds(r * plane, plane), dd, n:, :].reshape(plane * n, k) for r in range(halves)], axis=1
         )
         for to in range(rows):
             left = []
-            for r in range(rows):
-                at = pl.ds(r * per + to * few, few)
+            for r in range(halves):
+                at = pl.ds(r * plane + to * few, few)
                 both = jnp.concatenate(
                     [own_ref[at, dd, :n, :].reshape(few * n, k), other_ref[at, dd].reshape(few * n, k)], axis=0
                 )
                 left.append(both.astype(F32).T.astype(BF16))
             total = jnp.dot(right, jnp.concatenate(left, axis=0), preferred_element_type=F32) * scale
-            out_ref[pl.ds(to * per, per), dd] = total.astype(BF16).reshape(per, n, k)
+            out_ref[pl.ds(to * plane, plane), dd] = total.astype(BF16).reshape(plane, n, k)
 
 
 def back_kernel(m_ref, gate_ref, gain_ref, w_ref, out_hbm, rows_ref, sums_ref, out_ref, sems):
-    d, n, k = m_ref.shape
+    d2, n, k = m_ref.shape
+    d = d2 // 2
     pitch = n + 1
     step = 32
 
     def total(s, acc):
-        return acc + jnp.sum(m_ref[pl.ds(s * step, step)].astype(F32), axis=0)
+        for q in range(step):
+            at = s * step + q
+            m = m_ref[at].astype(F32) + m_ref[d + at].astype(F32)
+            rows_ref[pl.ds(at * pitch, n), :] = m
+            acc += m
+        return acc
 
     mean = lax.fori_loop(0, d // step, total, jnp.zeros((n, k), F32)) * (1.0 / d)
 
     def squares(s, acc):
-        centred = m_ref[pl.ds(s * step, step)].astype(F32) - mean
-        return acc + jnp.sum(centred * centred, axis=0)
+        for q in range(step):
+            centred = rows_ref[pl.ds((s * step + q) * pitch, n), :] - mean
+            acc += centred * centred
+        return acc
 
     power = lax.fori_loop(0, d // step, squares, jnp.zeros((n, k), F32)) * (1.0 / d)
     root = lax.rsqrt(power + 1e-05)
 
     def scaled(s, _):
         for q in range(step):
-            centred = m_ref[s * step + q].astype(F32) - mean
-            rows_ref[pl.ds((s * step + q) * pitch, n), :] = centred * root
+            at = pl.ds((s * step + q) * pitch, n)
+            rows_ref[at, :] = (rows_ref[at, :] - mean) * root
         return 0
 
     lax.fori_loop(0, d // step, scaled, 0)
@@ -190,15 +199,17 @@
         compiler_params=params,
         name="front",
     )(in_hbm(pair_array), in_hbm(in_gain.reshape(1, c)), in_hbm(left_weight), in_hbm(right_weight))
-    same_core = [[r * cols + q * 2 + core for r in range(rows) for q in range(cols // 2)] for core in range(2)]
     chips = rows * cols // 2
-
-    def exchange(x):
+    every = [[r * cols + q * 2 + core for r in range(rows) for q in range(cols // 2)] for core in range(2)]
+    of_half = [group[h * chips // 2 : (h + 1) * chips // 2] for group in every for h in range(2)]
+    per = d // (chips // 2)
+
+    def exchange(x, groups):
         return lax.all_to_all(
-            x, ("row", "col"), split_axis=0, concat_axis=0, tiled=True, axis_index_groups=same_core
+            x, ("row", "col"), split_axis=0, concat_axis=0, tiled=True, axis_index_groups=groups
         )
 
-    factors = exchange(factors).reshape(chips, 2, 2 * n, k)
+    factors = exchange(factors, of_half).reshape(chips // 2, per, 2 * n, k)
     other = lax.ppermute(factors[:, :, :n], "col", [(i, i ^ 1) for i in range(cols)])
     gate, gain, weight = pl.pallas_call(
         gate_kernel,
@@ -221,13 +232,13 @@
     factors, other, gate, gain, weight = lax.optimization_barrier((factors, other, gate, gain, weight))
     mixed = pl.pallas_call(
         functools.partial(middle_kernel, rows, (k * rows) ** -0.5),
-        out_shape=jax.ShapeDtypeStruct((chips, 2, n, k), BF16),
+        out_shape=jax.ShapeDtypeStruct((chips, per, n, k), BF16),
         in_specs=[VMEM] * 2,
         out_specs=VMEM,
         compiler_params=params,
         name="middle",
     )(factors, other)
-    mixed = exchange(mixed.reshape(d, n, k))
+    mixed = exchange(mixed.reshape(2 * d, n, k), every)
     return pl.pallas_call(
         back_kernel,
         out_shape=jax.ShapeDtypeStruct((k, n, c), BF16),

time: 71.1 us -> 69.5 us (0.977)
  blocking collectives: 61.1 us -> 59.6 us
    all_to_all x2, blocking collectives: 61.1 us -> 59.6 us  [exchange(): lax.all_to_all(x, ('row', 'col'), split_axis=0, concat_axis=0, tiled=True...]
where the time goes in v4:
time: 69.5 us; the launch traced here: 69.3 us
  blocking collectives  59.6 us (86%)
  Pallas kernels  6.95 us (10%)
  starting transfers between devices  2.6 us (4%)
    all_to_all x2, blocking collectives, exchange(): lax.all_to_all(x, ('row', 'col'), split_axis=0, concat_axis=0, tiled=True...  59.6 us
    ppermute x1, starting transfers between devices, body(): lax.ppermute(factors[:, :, :n], 'col', [(i, i ^ 1) for i in range(cols)])  2.6 us
    pallas_call x1, Pallas kernels, body(): pl.pallas_call(front_kernel, out_shape=(jax.ShapeDtypeStruct((k * n, c),...  2.32 us
    pallas_call x1, Pallas kernels, body(): pl.pallas_call(gate_kernel, out_shape=(jax.ShapeDtypeStruct((k * n, c), F...  2.1 us
    pallas_call x1, Pallas kernels, body(): pl.pallas_call(back_kernel, out_shape=jax.ShapeDtypeStruct((k, n, c), BF1...  1.73 us
  transfers between devices with their start and end apart: 1, of which 0 were waited for; matrix products, arithmetic and copies ran while one was open for 0% of the time, Pallas kernels for 3%

profile of v4, /device:TPU:1, one launch (start us, length us, event | category | flops | bytes accessed | tf_op | source)
XLA Modules:
  0.0 69.3 jit_solution(7094312344466261724)
XLA Ops:
  0.0 2.3 %front.1 = (bf16[2048,128]{1,0:T(8,128)(2,1)S(1)}, bf16[128,32,128]{2,1,0:T(8,128)(2,1)S(1)}) custom-call(bf16[128,16,128]{2,1,0:T(8,128)(2,1)} %x_hbm.1, f32[1,128]{1,0:T(1,128)} %bitcast.7, bf16[128,128]{1,0:T(8,128)(2,1)} %wl_hbm.1, bf16[128,128]{1,0:T(8,128)(2,1)} %wr_hbm.1), custom_call_target="tpu_custom_call" | custom-call | tf_op jit(solution)/shard_map/front/pallas_call | solution.py:182
  2.3 23.9 %all_to_all.10 = bf16[128,32,128]{2,1,0:T(8,128)(2,1)S(1)} all-to-all(bf16[128,32,128]{2,1,0:T(8,128)(2,1)S(1)} %get-tuple-element.15), channel_id=1, replica_groups={{0,2,4,6,8,10,12,14,16,18,20,22,24,26,28,30,32,34,36,38,40,42,44,46,48,..., dimensions={0} | all-to-all | bytes 2097152 | tf_op jit(solution)/shard_map/all_to_all | solution.py:208
  26.3 2.6 %collective-permute-start = (bf16[32,4,16,128]{3,2,1,0:T(8,128)(2,1)S(1)}, bf16[32,4,16,128]{3,2,1,0:T(8,128)(2,1)S(1)}, u32[]{:S(2)}, u32[]{:S(2)}) collective-permute-start(bf16[32,4,16,128]{3,2,1,0:T(8,128)(2,1)S(1)} %slice.4), channel_id=1, source_target_pairs={{0,1},{1,0},{2,3},{3,2},{4,5},{5,4},{6,7},{7,6},{8,9},{9,8},{10,11... | collective-permute-start | bytes 1572872 | tf_op jit(solution)/shard_map/ppermute | solution.py:213
  28.9 2.1 %gate.1 = (f32[2048,128]{1,0:T(8,128)S(1)}, f32[1,128]{1,0:T(1,128)S(1)}, bf16[128,128]{1,0:T(8,128)(2,1)S(1)}) custom-call(bf16[2048,128]{1,0:T(8,128)(2,1)S(1)} %get-tuple-element.16.ready_ref, bf16[128,128]{1,0:T(8,128)(2,1)} %gate_hbm.1, f32[1,128]{1,0:T(1,128)} %bitcast.8, bf16[128,128]{1,0:T(8,128)(2,1)} %w_hbm.1), custom_call_target="tpu_custom_call" | custom-call | flops 4000000000 | bytes 2097152 | tf_op jit(solution)/shard_map/gate/pallas_call | solution.py:214
  31.0 0.0 collective-permute-done.other_ref
  31.0 0.8 %middle.1 = bf16[64,4,16,128]{3,2,1,0:T(8,128)(2,1)S(1)} custom-call(bf16[32,4,32,128]{3,2,1,0:T(8,128)(2,1)S(1)} %bitcast.5, bf16[32,4,16,128]{3,2,1,0:T(8,128)(2,1)S(1)} %collective-permute-done.other_ref), custom_call_target="tpu_custom_call" | custom-call | tf_op jit(solution)/shard_map/middle/pallas_call | solution.py:233
  31.8 35.7 %all_to_all.11.m_ref = bf16[256,16,128]{2,1,0:T(8,128)(2,1)S(1)} all-to-all(bf16[256,16,128]{2,1,0:T(8,128)(2,1)S(1)} %bitcast.6), channel_id=1, replica_groups={{0,2,4,6,8,10,12,14,16,18,20,22,24,26,28,30,32,34,36,38,40,42,44,46,48,..., dimensions={0} | all-to-all | bytes 2097152 | tf_op jit(solution)/shard_map/all_to_all | solution.py:208
  67.5 1.7 %back.1 = bf16[128,16,128]{2,1,0:T(8,128)(2,1)} custom-call(bf16[256,16,128]{2,1,0:T(8,128)(2,1)S(1)} %all_to_all.11.m_ref, f32[2048,128]{1,0:T(8,128)S(1)} %get-tuple-element.22.gate_ref, f32[1,128]{1,0:T(1,128)S(1)} %get-tuple-element.23.gain_ref, bf16[128,128]{1,0:T(8,128)(2,1)S(1)} %get-tuple-element.24.w_ref), custom_call_target="tpu_custom_call" | custom-call | tf_op jit(solution)/shard_map/back/pallas_call | solution.py:242
  (1 shorter events, 0.0 us)
Async XLA Ops:
  26.3 4.7 %collective-permute-start = (bf16[32,4,16,128]{3,2,1,0:T(8,128)(2,1)S(1)}, bf16[32,4,16,128]{3,2,1,0:T(8,128)(2,1)S(1)}, u32[]{:S(2)}, u32[]{:S(2)}) collective-permute-start(bf16[32,4,16,128]{3,2,1,0:T(8,128)(2,1)S(1)} %slice.4), channel_id=1, source_target_pairs={{0,1},{1,0},{2,3},{3,2},{4,5},{5,4},{6,7},{7,6},{8,9},{9,8},{10,11... | collective-permute-start | bytes 1572872 | tf_op jit(solution)/shard_map/ppermute | solution.py:213

commit v5 on v4

v5 whole, which is shorter than its diff:
```python
import functools

import jax
import jax.numpy as jnp
from jax import lax
from jax.experimental import pallas as pl
from jax.experimental.pallas import tpu as pltpu
from jax.sharding import PartitionSpec as P

VMEM = pl.BlockSpec(memory_space=pltpu.VMEM)
HBM = pl.BlockSpec(memory_space=pltpu.HBM)
F32 = jnp.float32
BF16 = jnp.bfloat16
PIECES = 2


def nt(a, b):
    return lax.dot_general(a, b, (((1,), (1,)), ((), ())), preferred_element_type=F32)


def in_hbm(x):
    return pltpu.with_memory_space_constraint(x, pltpu.HBM)


def front_kernel(x_hbm, gain_hbm, wl_hbm, wr_hbm, gate_hbm, mid_gain_hbm, wo_hbm,
                 ready_ref, out_ref, gate_ref, mid_gain_ref, wo_ref,
                 x_ref, gain_ref, wl_ref, wr_ref, rows_ref, tiles_ref, sems):
    k, n, c = x_ref.shape
    d = wl_ref.shape[1]
    pitch, wide = n + 1, 2 * n + 1
    part = k // PIECES
    pieces = [(x_hbm.at[pl.ds(p * part, part)], x_ref.at[pl.ds(p * part, part)]) for p in range(PIECES)]
    weights = [(wl_hbm, wl_ref), (wr_hbm, wr_ref), (gain_hbm, gain_ref)]
    later = [(gate_hbm, gate_ref), (mid_gain_hbm, mid_gain_ref), (wo_hbm, wo_ref)]
    copies = [
        pltpu.make_async_copy(src, dst, sems.at[at]) for at, (src, dst) in enumerate(weights + pieces + later)
    ]
    for copy in copies:
        copy.start()
    for copy in copies[:3]:
        copy.wait()
    w = jnp.concatenate([wl_ref[...].astype(F32).T, wr_ref[...].astype(F32).T], axis=0).astype(BF16)
    gain = gain_ref[...]
    for p in range(PIECES):
        copies[3 + p].wait()
        x = x_ref[pl.ds(p * part, part)].reshape(part * n, c).astype(F32)
        centred = x - jnp.mean(x, axis=-1, keepdims=True)
        power = jnp.mean(centred * centred, axis=-1, keepdims=True)
        ready = (centred * lax.rsqrt(power + 1e-05) * gain).astype(BF16)
        ready_ref[pl.ds(p * part * n, part * n), :] = ready
        rows = ready.astype(F32)
        for q in range(part):
            rows_ref[pl.ds((p * part + q) * pitch, n), :] = rows[q * n : (q + 1) * n]
    for i in range(n):
        both = nt(w, rows_ref[pl.ds(i, k, stride=pitch), :].astype(BF16))
        tiles_ref[pl.ds(i, d, stride=wide), :] = both[:d]
        tiles_ref[pl.ds(n + i, d, stride=wide), :] = both[d:]
    for q in range(d):
        out_ref[q] = tiles_ref[pl.ds(q * wide, 2 * n), :].astype(BF16)
    for copy in copies[3 + PIECES :]:
        copy.wait()


def gate_kernel(ready_ref, gate_ref, out_ref):
    out_ref[...] = jax.nn.sigmoid(jnp.dot(ready_ref[...], gate_ref[...], preferred_element_type=F32))


def middle_kernel(rows, scale, own_ref, other_ref, out_ref):
    chips, per, n, k = other_ref.shape
    halves = rows // 2
    plane = chips // halves
    few = plane // rows
    for dd in range(per):
        right = jnp.concatenate(
            [own_ref[pl.ds(r * plane, plane), dd, n:, :].reshape(plane * n, k) for r in range(halves)], axis=1
        )
        lines = []
        for to in range(rows):
            left = []
            for r in range(halves):
                at = pl.ds(r * plane + to * few, few)
                both = jnp.concatenate(
                    [own_ref[at, dd, :n, :].reshape(few * n, k), other_ref[at, dd].reshape(few * n, k)], axis=0
                )
                left.append(both.T)
            lines.append(jnp.concatenate(left, axis=0))
        for to in range(0, rows, 2):
            total = jnp.dot(right, jnp.concatenate(lines[to : to + 2], axis=1), preferred_element_type=F32) * scale
            for q in range(2):
                tile = total[:, q * k : (q + 1) * k].astype(BF16).reshape(plane, n, k)
                out_ref[pl.ds((to + q) * plane, plane), dd] = tile


def back_kernel(m_ref, gate_ref, gain_ref, w_ref, out_hbm, rows_ref, sums_ref, out_ref, sems):
    d2, n, k = m_ref.shape
    d = d2 // 2
    pitch = n + 1
    def over_channels(term):
        parts = [jnp.zeros((n, k), F32) for _ in range(4)]
        for at in range(d):
            parts[at % 4] += term(at)
        return (parts[0] + parts[1]) + (parts[2] + parts[3])

    def value(at):
        m = m_ref[at].astype(F32) + m_ref[d + at].astype(F32)
        rows_ref[pl.ds(at * pitch, n), :] = m
        return m

    mean = over_channels(value) * (1.0 / d)

    def square(at):
        centred = rows_ref[pl.ds(at * pitch, n), :] - mean
        return centred * centred

    root = lax.rsqrt(over_channels(square) * (1.0 / d) + 1e-05)
    for at in range(d):
        line = pl.ds(at * pitch, n)
        rows_ref[line, :] = (rows_ref[line, :] - mean) * root
    w = w_ref[...]
    gain = gain_ref[...]
    core = lax.rem(lax.axis_index("col"), 2)
    for j in range(n):
        t = (rows_ref[pl.ds(j, d, stride=pitch), :].T * gain).astype(BF16)
        sums = jnp.dot(t, w, preferred_element_type=F32)
        for h in range(2):
            for q in range(k // (2 * n)):
                at = (2 * q + (1 - core if h else core)) * n * pitch + j
                block = h * (k // 2) + q * n
                sums_ref[pl.ds(at, n, stride=pitch), :] = sums[block : block + n]
    part = k // PIECES
    copies = []
    for p in range(PIECES):
        for at in range(p * part, (p + 1) * part):
            out_ref[at] = (sums_ref[pl.ds(at * pitch, n), :] * gate_ref[pl.ds(at * n, n), :]).astype(BF16)
        copy = pltpu.make_async_copy(
            out_ref.at[pl.ds(p * part, part)], out_hbm.at[pl.ds(p * part, part)], sems.at[p]
        )
        copy.start()
        copies.append(copy)
    for copy in copies:
        copy.wait()


def body(pair_array, in_gain, left_weight, right_weight, mid_gain, out_weight, out_gate):
    k, n, c = pair_array.shape
    d = left_weight.shape[1]
    rows, cols = lax.axis_size("row"), lax.axis_size("col")
    params = pltpu.CompilerParams(vmem_limit_bytes=32 << 20)
    ready, factors, gate_weight, gain, weight = pl.pallas_call(
        front_kernel,
        out_shape=(
            jax.ShapeDtypeStruct((k * n, c), BF16),
            jax.ShapeDtypeStruct((d, 2 * n, k), BF16),
            jax.ShapeDtypeStruct((c, c), BF16),
            jax.ShapeDtypeStruct((1, d), F32),
            jax.ShapeDtypeStruct((d, c), BF16),
        ),
        in_specs=[HBM] * 7,
        out_specs=(VMEM,) * 5,
        scratch_shapes=[
            pltpu.VMEM((k, n, c), BF16),
            pltpu.VMEM((1, c), F32),
            pltpu.VMEM((c, d), BF16),
            pltpu.VMEM((c, d), BF16),
            pltpu.VMEM((k * (n + 1), c), F32),
            pltpu.VMEM((d * (2 * n + 1), k), F32),
            pltpu.SemaphoreType.DMA((PIECES + 6,)),
        ],
        compiler_params=params,
        name="front",
    )(
        in_hbm(pair_array),
        in_hbm(in_gain.reshape(1, c)),
        in_hbm(left_weight),
        in_hbm(right_weight),
        in_hbm(out_gate),
        in_hbm(mid_gain.reshape(1, d)),
        in_hbm(out_weight),
    )
    chips = rows * cols // 2
    every = [[r * cols + q * 2 + core for r in range(rows) for q in range(cols // 2)] for core in range(2)]
    of_half = [group[h * chips // 2 : (h + 1) * chips // 2] for group in every for h in range(2)]
    per = d // (chips // 2)

    def exchange(x, groups):
        return lax.all_to_all(
            x, ("row", "col"), split_axis=0, concat_axis=0, tiled=True, axis_index_groups=groups
        )

    factors = exchange(factors, of_half).reshape(chips // 2, per, 2 * n, k)
    other = lax.ppermute(factors[:, :, :n], "col", [(i, i ^ 1) for i in range(cols)])
    gate = pl.pallas_call(
        gate_kernel,
        out_shape=jax.ShapeDtypeStruct((k * n, c), F32),
        in_specs=[VMEM] * 2,
        out_specs=VMEM,
        compiler_params=params,
        cost_estimate=pl.CostEstimate(flops=4_000_000_000, bytes_accessed=2 << 20, transcendentals=k * n * c),
        name="gate",
    )(ready, gate_weight)
    factors, other, gate = lax.optimization_barrier((factors, other, gate))
    mixed = pl.pallas_call(
        functools.partial(middle_kernel, rows, (k * rows) ** -0.5),
        out_shape=jax.ShapeDtypeStruct((chips, per, n, k), BF16),
        in_specs=[VMEM] * 2,
        out_specs=VMEM,
        compiler_params=params,
        name="middle",
    )(factors, other)
    mixed = exchange(mixed.reshape(2 * d, n, k), every)
    return pl.pallas_call(
        back_kernel,
        out_shape=jax.ShapeDtypeStruct((k, n, c), BF16),
        in_specs=[VMEM] * 4,
        out_specs=HBM,
        scratch_shapes=[
            pltpu.VMEM((d * (n + 1), k), F32),
            pltpu.VMEM((k * (n + 1), c), F32),
            pltpu.VMEM((k, n, c), BF16),
            pltpu.SemaphoreType.DMA((PIECES,)),
        ],
        compiler_params=params,
        name="back",
    )(mixed, gate, gain, weight)


def solution(mesh):
    return jax.shard_map(
        body,
        mesh=mesh,
        in_specs=(
            P(("site", "row"), "col", None),
            P(),
            P("site", None),
            P("site", None),
            P(),
            P("site", None),
            P("site", None),
        ),
        out_specs=P(("site", "row"), "col", None),
        check_vma=False,
    )
```

time: 69.5 us -> 68.3 us (0.983)
  Pallas kernels: 6.95 us -> 4.73 us
  waiting for transfers between devices: 0.01 us -> 1.24 us
    pallas_call x1, Pallas kernels: 2.1 us -> 0.29 us  [body(): pl.pallas_call(gate_kernel, out_shape=jax.ShapeDtypeStruct((k * n, c), F3...]
    ppermute x1, waiting for transfers between devices: 0.01 us -> 1.24 us  [body(): lax.ppermute(factors[:, :, :n], 'col', [(i, i ^ 1) for i in range(cols)])]
  transfers between devices with their start and end apart: 1 -> 1, of which waited for: 0 -> 1; matrix products, arithmetic and copies ran while one was open for 0% -> 0% of each run, Pallas kernels for 3% -> 0%
where the time goes in v5:
time: 68.3 us; the launch traced here: 67.9 us
  blocking collectives  59.3 us (87%)
  Pallas kernels  4.73 us (7%)
  starting transfers between devices  2.6 us (4%)
  waiting for transfers between devices  1.24 us (2%)
    all_to_all x2, blocking collectives, exchange(): lax.all_to_all(x, ('row', 'col'), split_axis=0, concat_axis=0, tiled=True...  59.3 us
    ppermute x1, starting transfers between devices, body(): lax.ppermute(factors[:, :, :n], 'col', [(i, i ^ 1) for i in range(cols)])  2.6 us
    pallas_call x1, Pallas kernels, body(): pl.pallas_call(front_kernel, out_shape=(jax.ShapeDtypeStruct((k * n, c),...  2.3 us
    pallas_call x1, Pallas kernels, body(): pl.pallas_call(back_kernel, out_shape=jax.ShapeDtypeStruct((k, n, c), BF1...  1.61 us
  transfers between devices with their start and end apart: 1, of which 1 were waited for; matrix products, arithmetic and copies ran while one was open for 0% of the time, Pallas kernels for 0%

profile of v5, /device:TPU:1, one launch (start us, length us, event | category | flops | bytes accessed | tf_op | source)
XLA Modules:
  0.0 67.9 jit_solution(2246465517689802407)
XLA Ops:
  0.0 2.3 %front.1 = (bf16[2048,128]{1,0:T(8,128)(2,1)S(1)}, bf16[128,32,128]{2,1,0:T(8,128)(2,1)S(1)}, bf16[128,128]{1,0:T(8,128)(2,1)S(1)}, f32[1,128]{1,0:T(1,128)S(1)}, bf16[128,128]{1,0:T(8,128)(2,1)S(1)}) custom-call(bf16[128,16,128]{2,1,0:T(8,128)(2,1)} %x_hbm.1, f32[1,128]{1,0:T(1,128)} %bitcast.7, bf16[128,128]{1,0:T(8,128)(2,1)} %wl_hbm.1, ...), custom_call_target="tpu_custom_call" | custom-call | tf_op jit(solution)/shard_map/front/pallas_call | solution.py:149
  2.3 23.9 %all_to_all.10 = bf16[128,32,128]{2,1,0:T(8,128)(2,1)S(1)} all-to-all(bf16[128,32,128]{2,1,0:T(8,128)(2,1)S(1)} %get-tuple-element.13), channel_id=1, replica_groups={{0,2,4,6,8,10,12,14,16,18,20,22,24,26,28,30,32,34,36,38,40,42,44,46,48,..., dimensions={0} | all-to-all | bytes 2097152 | tf_op jit(solution)/shard_map/all_to_all | solution.py:186
  26.3 2.6 %collective-permute-start = (bf16[32,4,16,128]{3,2,1,0:T(8,128)(2,1)S(1)}, bf16[32,4,16,128]{3,2,1,0:T(8,128)(2,1)S(1)}, u32[]{:S(2)}, u32[]{:S(2)}) collective-permute-start(bf16[32,4,16,128]{3,2,1,0:T(8,128)(2,1)S(1)} %slice.4), channel_id=1, source_target_pairs={{0,1},{1,0},{2,3},{3,2},{4,5},{5,4},{6,7},{7,6},{8,9},{9,8},{10,11... | collective-permute-start | bytes 1572872 | tf_op jit(solution)/shard_map/ppermute | solution.py:191
  28.9 0.3 gate.1.gate_ref
  29.2 1.2 %collective-permute-done.other_ref = bf16[32,4,16,128]{3,2,1,0:T(8,128)(2,1)S(1)} collective-permute-done((bf16[32,4,16,128]{3,2,1,0:T(8,128)(2,1)S(1)}, bf16[32,4,16,128]{3,2,1,0:T(8,128)(2,1)S(1)}, u32[]{:S(2)}, u32[]{:S(2)}) %collective-permute-start) | collective-permute-done | bytes 524320 | tf_op jit(solution)/shard_map/ppermute | solution.py:191
  30.4 0.5 middle.1
  31.0 35.3 %all_to_all.11.m_ref = bf16[256,16,128]{2,1,0:T(8,128)(2,1)S(1)} all-to-all(bf16[256,16,128]{2,1,0:T(8,128)(2,1)S(1)} %bitcast.6), channel_id=1, replica_groups={{0,2,4,6,8,10,12,14,16,18,20,22,24,26,28,30,32,34,36,38,40,42,44,46,48,..., dimensions={0} | all-to-all | bytes 2097152 | tf_op jit(solution)/shard_map/all_to_all | solution.py:186
  66.3 1.6 %back.1 = bf16[128,16,128]{2,1,0:T(8,128)(2,1)} custom-call(bf16[256,16,128]{2,1,0:T(8,128)(2,1)S(1)} %all_to_all.11.m_ref, f32[2048,128]{1,0:T(8,128)S(1)} %gate.1.gate_ref, f32[1,128]{1,0:T(1,128)S(1)} %get-tuple-element.19.gain_ref, bf16[128,128]{1,0:T(8,128)(2,1)S(1)} %get-tuple-element.20.w_ref), custom_call_target="tpu_custom_call" | custom-call | tf_op jit(solution)/shard_map/back/pallas_call | solution.py:211
  (1 shorter events, 0.0 us)
Async XLA Ops:
  26.3 4.1 %collective-permute-start = (bf16[32,4,16,128]{3,2,1,0:T(8,128)(2,1)S(1)}, bf16[32,4,16,128]{3,2,1,0:T(8,128)(2,1)S(1)}, u32[]{:S(2)}, u32[]{:S(2)}) collective-permute-start(bf16[32,4,16,128]{3,2,1,0:T(8,128)(2,1)S(1)} %slice.4), channel_id=1, source_target_pairs={{0,1},{1,0},{2,3},{3,2},{4,5},{5,4},{6,7},{7,6},{8,9},{9,8},{10,11... | collective-permute-start | bytes 1572872 | tf_op jit(solution)/shard_map/ppermute | solution.py:191
